TPU v7x, 32 devices: a whole 2x2x4 slice. The times are simulated.
32 devices in a mesh: dp: 32 (over z, y, x, core).
Axes of the slice: x: 2, y: 2, z: 4, core: 2. Of those that a mesh axis runs over, the one named last changes fastest.
Arguments:
- block_input: bfloat16 [32768, 640], P('dp'), may hold values from -6 to 6
- out_cotangent: bfloat16 [32768, 640], P('dp'), may hold values from -6 to 6
- segment_ids: int32 [32768], P('dp'), may hold values from 0 to 1023, as said below
- positions: int32 [32768], P('dp'), may hold values from 0 to 1023, as said below
- tile_count: int32 [32], P('dp'), may hold values from 1 to 8, as said below
- qkv_weight: float32 [640, 1536], P('dp'), may hold values from -0.25 to 0.25
- qkv_first: float32 [640, 1536], P('dp'), may hold values from -6 to 6
- qkv_second: float32 [640, 1536], P('dp'), may hold values from 0.01 to 1
- out_weight: float32 [1024, 640], P('dp'), may hold values from -0.1875 to 0.1875
- out_first: float32 [1024, 640], P('dp'), may hold values from -6 to 6
- out_second: float32 [1024, 640], P('dp'), may hold values from 0.01 to 1
- gate_up_weight: float32 [640, 4096], P('dp'), may hold values from -0.25 to 0.25
- gate_up_first: float32 [640, 4096], P('dp'), may hold values from -6 to 6
- gate_up_second: float32 [640, 4096], P('dp'), may hold values from 0.01 to 1
- down_weight: float32 [2048, 640], P('dp'), may hold values from -0.125 to 0.125
- down_first: float32 [2048, 640], P('dp'), may hold values from -6 to 6
- down_second: float32 [2048, 640], P('dp'), may hold values from 0.01 to 1
- norm_scales: float32 [3072], P('dp'), may hold values from -0.6 to 0.6
- norm_first: float32 [3072], P('dp'), may hold values from -6 to 6
- norm_second: float32 [3072], P('dp'), may hold values from 0.01 to 1
Outputs:
- block_output: bfloat16 [32768, 640], P('dp')
- input_grad: float32 [32768, 640], P('dp')
- qkv_grad: float32 [640, 1536], P('dp')
- out_grad: float32 [1024, 640], P('dp')
- gate_up_grad: float32 [640, 4096], P('dp')
- down_grad: float32 [2048, 640], P('dp')
- norm_grad: float32 [3072], P('dp')
- qkv_new: float32 [640, 1536], P('dp')
- out_new: float32 [1024, 640], P('dp')
- gate_up_new: float32 [640, 4096], P('dp')
- down_new: float32 [2048, 640], P('dp')
- norms_new: float32 [3072], P('dp')
- qkv_first_new: float32 [640, 1536], P('dp')
- out_first_new: float32 [1024, 640], P('dp')
- gate_up_first_new: float32 [640, 4096], P('dp')
- down_first_new: float32 [2048, 640], P('dp')
- norm_first_new: float32 [3072], P('dp')
- qkv_second_new: float32 [640, 1536], P('dp')
- out_second_new: float32 [1024, 640], P('dp')
- gate_up_second_new: float32 [640, 4096], P('dp')
- down_second_new: float32 [2048, 640], P('dp')
- norm_second_new: float32 [3072], P('dp')
Inputs may be any that keep to these rules, and one draw needn't show every extreme that they name: `tile_count`: how many of a device's 8 tiles hold tokens; the rows of the remaining tiles are padding. `segment_ids`: within each device's 1024 slots: 0 at the first slot, never falling, rising by at most one from slot to slot; no sequence spans two devices. `positions`: within each device: 0 at every slot where segment_ids changes (and at the device's first slot), else one more than at the slot before.
All inputs are finite; a program needn't handle non-finite values.
Results may differ from a plain program's by a relative error of at most 0.02.
The roundings to bfloat16 on the way count: a program that leaves them out, or rounds other values in their place, can miss the bound.
Values may be sent and summed in bfloat16 or wider, within the bound.
A program may use at most 192 MiB of HBM per device.

v0:
```python
import functools
import math

import numpy as np

import jax
import jax.numpy as jnp
from jax import lax
from jax.experimental import pallas as pl
from jax.experimental.pallas import tpu as pltpu
from jax.sharding import PartitionSpec as P

D = 640
HQ = 4
HD = 256
FF = 2048
WIN = 512
TILE = 128


norm_eps = 1e-06
rope_base = 10000.0
beta_one = 0.9
beta_two = 0.999
adam_eps = 1e-08
learn_rate = 0.02
weight_decay = 0.1
adam_step = 3


def rms_scale(values, scales):
    mean_square = jnp.mean(values * values, axis=-1, keepdims=True)
    return values * lax.rsqrt(mean_square + norm_eps) * (1.0 + scales)


def gelu_tanh(values):
    inner_term = 0.7978845608028654 * (values + 0.044715 * values * values * values)
    return 0.5 * values * (1.0 + jnp.tanh(inner_term))


def gated_unit(gate_act, up_act):
    return gelu_tanh(gate_act) * up_act


def rotate(values, cosine, sine_table):
    half_dim = values.shape[-1] // 2
    front_half = values[..., :half_dim]
    back_half = values[..., half_dim:]
    return jnp.concatenate(
        [
            front_half * cosine - back_half * sine_table,
            back_half * cosine + front_half * sine_table,
        ],
        axis=-1,
    )


def rope_tables(positions, head_dim):
    exponent = jnp.arange(head_dim // 2, dtype=jnp.float32) * (2.0 / head_dim)
    frequency = jnp.power(jnp.float32(rope_base), -exponent)
    angles = positions.astype(jnp.float32)[:, None] * frequency[None, :]
    return (jnp.cos(angles)[:, None, :], jnp.sin(angles)[:, None, :])


def qk_prepare(query_raw, key_raw, q_scale, k_scale, cosine, sine_table):
    return (
        rotate(rms_scale(query_raw, q_scale), cosine, sine_table),
        rotate(rms_scale(key_raw, k_scale), cosine, sine_table),
    )


def contract(form, left, right):
    return jnp.einsum(form, left, right, preferred_element_type=jnp.float32)


def window_mask(block_index, window, segment_pad, live_pad):
    start_row = block_index * window
    query_rows = start_row + jnp.arange(window, dtype=jnp.int32)
    key_rows = start_row - window + jnp.arange(2 * window, dtype=jnp.int32)
    query_seg = segment_pad[start_row + window : start_row + 2 * window]
    key_seg = segment_pad[start_row : start_row + 2 * window]
    query_live = live_pad[start_row + window : start_row + 2 * window]
    key_live = live_pad[start_row : start_row + 2 * window]
    diagonal = key_rows[None, :] == query_rows[:, None]
    earlier = (key_rows[None, :] < query_rows[:, None]) & (
        query_rows[:, None] - key_rows[None, :] < window
    )
    same_seq = (query_seg[:, None] == key_seg[None, :]) & query_live[:, None] & key_live[None, :]
    return diagonal | earlier & same_seq


def front_pad(values, window):
    return jnp.concatenate([jnp.zeros((window,) + values.shape[1:], values.dtype), values], axis=0)


def attend_forward(query_bf, key_bf, value_bf, segment_pad, live_pad):
    row_count = query_bf.shape[0]
    score_scale = HD ** (-0.5)
    key_padded = front_pad(key_bf, WIN)
    value_padded = front_pad(value_bf, WIN)
    out_blocks = []
    log_blocks = []
    for block_index in range(row_count // WIN):
        start_row = block_index * WIN
        allowed = window_mask(block_index, WIN, segment_pad, live_pad)
        query_block = query_bf[start_row : start_row + WIN]
        key_block = key_padded[start_row : start_row + 2 * WIN]
        value_block = value_padded[start_row : start_row + 2 * WIN]
        scores = contract("qhd,kd->hqk", query_block, key_block) * score_scale
        exp_scores = jnp.where(allowed[None], jnp.exp(scores), 0.0)
        exp_total = jnp.sum(exp_scores, axis=-1)
        probs_bf = (exp_scores / exp_total[..., None]).astype(jnp.bfloat16)
        out_blocks.append(contract("hqk,kd->qhd", probs_bf, value_block).reshape(WIN, HQ * HD))
        log_blocks.append(jnp.log(exp_total))
    return (jnp.concatenate(out_blocks, axis=0), jnp.concatenate(log_blocks, axis=1))


def attend_backward(
    query_bf, key_bf, value_bf, attn_bf, dattn_bf, log_total, segment_pad, live_pad
):
    row_count = query_bf.shape[0]
    score_scale = HD ** (-0.5)
    key_padded = front_pad(key_bf, WIN)
    value_padded = front_pad(value_bf, WIN)
    attn_heads = attn_bf.reshape(row_count, HQ, HD)
    dattn_heads = dattn_bf.reshape(row_count, HQ, HD)
    delta_rows = jnp.sum(dattn_heads.astype(jnp.float32) * attn_heads.astype(jnp.float32), axis=-1)
    key_grad = jnp.zeros((row_count + WIN, HD), jnp.float32)
    value_grad = jnp.zeros((row_count + WIN, HD), jnp.float32)
    query_parts = []
    for block_index in range(row_count // WIN):
        start_row = block_index * WIN
        allowed = window_mask(block_index, WIN, segment_pad, live_pad)
        query_block = query_bf[start_row : start_row + WIN]
        key_block = key_padded[start_row : start_row + 2 * WIN]
        value_block = value_padded[start_row : start_row + 2 * WIN]
        dout_block = dattn_heads[start_row : start_row + WIN]
        scores = contract("qhd,kd->hqk", query_block, key_block) * score_scale
        probs = jnp.where(
            allowed[None], jnp.exp(scores - log_total[:, start_row : start_row + WIN, None]), 0.0
        )
        probs_bf = probs.astype(jnp.bfloat16)
        value_grad = value_grad.at[start_row : start_row + 2 * WIN].add(
            contract("hqk,qhd->kd", probs_bf, dout_block)
        )
        dprobs = contract("qhd,kd->hqk", dout_block, value_block)
        dscores = (
            probs * (dprobs - delta_rows[start_row : start_row + WIN].T[:, :, None]) * score_scale
        )
        dscores_bf = dscores.astype(jnp.bfloat16)
        query_parts.append(contract("hqk,kd->qhd", dscores_bf, key_block))
        key_grad = key_grad.at[start_row : start_row + 2 * WIN].add(
            contract("hqk,qhd->kd", dscores_bf, query_block)
        )
    return (jnp.concatenate(query_parts, axis=0), key_grad[WIN:], value_grad[WIN:])


def forward_pass(attn_full, ffn_full, block_input, segment_ids, positions, live_rows):
    qkv_w, out_w, norm_bf = attn_full
    gate_up_w, down_w = ffn_full
    norm_values = norm_bf.astype(jnp.float32)
    row_count = block_input.shape[0]
    resid_in = block_input.astype(jnp.float32)
    normed = rms_scale(resid_in, norm_values[0:D]).astype(jnp.bfloat16)
    qkv_proj = jnp.dot(normed, qkv_w, preferred_element_type=jnp.float32)
    query_raw = qkv_proj[:, : HQ * HD].reshape(row_count, HQ, HD)
    key_raw = qkv_proj[:, HQ * HD : (HQ + 1) * HD].reshape(row_count, 1, HD)
    value_bf = qkv_proj[:, (HQ + 1) * HD :].astype(jnp.bfloat16)
    cosine, sine_table = rope_tables(positions, HD)
    query_rot, key_rot = qk_prepare(
        query_raw,
        key_raw,
        norm_values[4 * D : 4 * D + HD],
        norm_values[4 * D + HD : 4 * D + 2 * HD],
        cosine,
        sine_table,
    )
    query_bf = query_rot.astype(jnp.bfloat16)
    key_bf = key_rot[:, 0, :].astype(jnp.bfloat16)
    segment_pad = front_pad(segment_ids, WIN)
    position_pad = front_pad(positions, WIN)
    live_pad = front_pad(live_rows, WIN)
    attn_out, log_total = attend_forward(query_bf, key_bf, value_bf, segment_pad, live_pad)
    attn_bf = attn_out.astype(jnp.bfloat16)
    attn_proj = jnp.dot(attn_bf, out_w, preferred_element_type=jnp.float32)
    mid_resid = resid_in + rms_scale(attn_proj, norm_values[D : 2 * D])
    ffn_in = rms_scale(mid_resid, norm_values[2 * D : 3 * D]).astype(jnp.bfloat16)
    gate_up = jnp.dot(ffn_in, gate_up_w, preferred_element_type=jnp.float32)
    gate_act = gate_up[:, :FF]
    up_act = gate_up[:, FF:]
    hidden = gated_unit(gate_act, up_act).astype(jnp.bfloat16)
    down_act = jnp.dot(hidden, down_w, preferred_element_type=jnp.float32)
    block_output = (mid_resid + rms_scale(down_act, norm_values[3 * D : 4 * D])).astype(
        jnp.bfloat16
    )
    attn_saved = (
        resid_in,
        normed,
        query_raw,
        key_raw,
        query_bf,
        key_bf,
        value_bf,
        cosine,
        sine_table,
        segment_pad,
        position_pad,
        live_pad,
        attn_bf,
        log_total,
        attn_proj,
    )
    ffn_saved = (mid_resid, ffn_in, gate_act, up_act, hidden, down_act)
    return (block_output, attn_saved, ffn_saved)


def ffn_backward(ffn_back, norm_values, ffn_saved, grad_out):
    gate_up_w, down_w = ffn_back
    mid_resid, ffn_in, gate_act, up_act, hidden, down_act = ffn_saved
    d_down, out_scale_grad = jax.vjp(rms_scale, down_act, norm_values[3 * D : 4 * D])[1](grad_out)
    d_down_bf = d_down.astype(jnp.bfloat16)
    d_hidden = jnp.dot(d_down_bf, down_w.T, preferred_element_type=jnp.float32)
    down_term = jnp.dot(hidden.T, d_down_bf, preferred_element_type=jnp.float32)
    d_gate, d_up = jax.vjp(gated_unit, gate_act, up_act)[1](d_hidden)
    d_gate_up = jnp.concatenate([d_gate, d_up], axis=1).astype(jnp.bfloat16)
    d_ffn_in = jnp.dot(d_gate_up, gate_up_w.T, preferred_element_type=jnp.float32)
    gate_up_term = jnp.dot(ffn_in.T, d_gate_up, preferred_element_type=jnp.float32)
    d_mid_part, ffn_scale_grad = jax.vjp(rms_scale, mid_resid, norm_values[2 * D : 3 * D])[1](
        d_ffn_in
    )
    return (grad_out + d_mid_part, gate_up_term, down_term, ffn_scale_grad, out_scale_grad)


def attn_backward(attn_back, attn_saved, d_mid):
    qkv_w, out_w, norm_bf = attn_back
    norm_values = norm_bf.astype(jnp.float32)
    (
        resid_in,
        normed,
        query_raw,
        key_raw,
        query_bf,
        key_bf,
        value_bf,
        cosine,
        sine_table,
        segment_pad,
        position_pad,
        live_pad,
        attn_bf,
        log_total,
        attn_proj,
    ) = attn_saved
    row_count = resid_in.shape[0]
    d_proj, post_scale_grad = jax.vjp(rms_scale, attn_proj, norm_values[D : 2 * D])[1](d_mid)
    d_proj_bf = d_proj.astype(jnp.bfloat16)
    out_term = jnp.dot(attn_bf.T, d_proj_bf, preferred_element_type=jnp.float32)
    dattn_bf = jnp.dot(d_proj_bf, out_w.T, preferred_element_type=jnp.float32).astype(jnp.bfloat16)
    d_query, d_key, d_value = attend_backward(
        query_bf, key_bf, value_bf, attn_bf, dattn_bf, log_total, segment_pad, live_pad
    )

    def prepare(query_in, key_in, q_in, k_in):
        return qk_prepare(query_in, key_in, q_in, k_in, cosine, sine_table)

    d_query_raw, d_key_raw, query_scale_grad, key_scale_grad = jax.vjp(
        prepare,
        query_raw,
        key_raw,
        norm_values[4 * D : 4 * D + HD],
        norm_values[4 * D + HD : 4 * D + 2 * HD],
    )[1]((d_query, d_key[:, None, :]))
    d_qkv = jnp.concatenate(
        [d_query_raw.reshape(row_count, HQ * HD), d_key_raw.reshape(row_count, HD), d_value], axis=1
    ).astype(jnp.bfloat16)
    d_normed = jnp.dot(d_qkv, qkv_w.T, preferred_element_type=jnp.float32)
    qkv_term = jnp.dot(normed.T, d_qkv, preferred_element_type=jnp.float32)
    d_input_part, in_scale_grad = jax.vjp(rms_scale, resid_in, norm_values[0:D])[1](d_normed)
    return (
        d_mid + d_input_part,
        qkv_term,
        out_term,
        in_scale_grad,
        post_scale_grad,
        query_scale_grad,
        key_scale_grad,
    )


def adam_update(weight, grad, first_moment, second_moment):
    first_new = beta_one * first_moment + (1.0 - beta_one) * grad
    second_new = beta_two * second_moment + (1.0 - beta_two) * grad * grad
    corr_one = 1.0 - beta_one**adam_step
    corr_two = 1.0 - beta_two**adam_step
    step_dir = (
        first_new / corr_one / (jnp.sqrt(second_new / corr_two) + adam_eps) + weight_decay * weight
    )
    return (weight - learn_rate * step_dir, first_new, second_new)


LOGICAL = pl.DeviceIdType.LOGICAL
ALL = slice(None)
SLOTS = 10


def grid_dims(count):
    return (count // 8, 2, 2, 2)


def my_place(dims):
    index = lax.axis_index("dp")
    core = lax.rem(index, dims[3])
    index = lax.div(index, dims[3])
    x = lax.rem(index, dims[2])
    index = lax.div(index, dims[2])
    return (lax.div(index, dims[1]), lax.rem(index, dims[1]), x, core)


def device_at(dims, z, y, x, core):
    return ((z * dims[1] + y) * dims[2] + x) * dims[3] + core


def enter(dims, place):
    z, y, x, core = place
    barrier = pltpu.get_barrier_semaphore()
    peers = [device_at(dims, lax.rem(z + k, dims[0]), y, x, core) for k in range(1, dims[0])]
    peers.append(device_at(dims, z, 1 - y, x, core))
    peers.append(device_at(dims, z, y, 1 - x, core))
    peers.append(device_at(dims, z, y, x, 1 - core))
    for peer in peers:
        pl.semaphore_signal(barrier, inc=1, device_id=peer, device_id_type=LOGICAL)
    pl.semaphore_wait(barrier, len(peers))


class Link:
    def __init__(self, dims, place, send_sems, recv_sems, base):
        self.dims, self.place = dims, place
        self.send_sems, self.recv_sems, self.base = send_sems, recv_sems, base
        self.pending = []

    def copy(self, src, dst, target, slot):
        return pltpu.make_async_remote_copy(
            src_ref=src,
            dst_ref=dst,
            send_sem=self.send_sems.at[self.base + slot],
            recv_sem=self.recv_sems.at[self.base + slot],
            device_id=target,
            device_id_type=LOGICAL,
        )

    def send(self, src, dst, target, slot):
        copy = self.copy(src, dst, target, slot)
        copy.start()
        self.pending.append(copy)

    def finish(self):
        for copy in self.pending:
            copy.wait_send()
        self.pending = []

    def z_peer(self, k):
        z, y, x, core = self.place
        return device_at(self.dims, lax.rem(z + k, self.dims[0]), y, x, core)

    def y_peer(self):
        z, y, x, core = self.place
        return device_at(self.dims, z, 1 - y, x, core)

    def x_peer(self):
        z, y, x, core = self.place
        return device_at(self.dims, z, y, 1 - x, core)

    def core_peer(self):
        z, y, x, core = self.place
        return device_at(self.dims, z, y, x, 1 - core)


class Gather(Link):
    def __init__(self, dims, place, view, swap, send_sems, recv_sems, base):
        super().__init__(dims, place, send_sems, recv_sems, base)
        self.view, self.swap = view, swap

    def plan(self, stage):
        z, y, x, core = self.place
        count = self.dims[0]
        view = self.view
        if stage == 0:
            return [
                (view(z, y, x, core), self.z_peer(k), k - 1, view(lax.rem(z + count - k, count), y, x, core))
                for k in range(1, count)
            ]
        slot = count + stage
        near, far = (self.y_peer(), self.x_peer()) if self.swap else (self.x_peer(), self.y_peer())
        if stage == 1:
            got = view(ALL, 1 - y, x, core) if self.swap else view(ALL, y, 1 - x, core)
            return [(view(ALL, y, x, core), near, slot, got)]
        if stage == 2:
            mine = view(ALL, ALL, x, core) if self.swap else view(ALL, y, ALL, core)
            got = view(ALL, ALL, 1 - x, core) if self.swap else view(ALL, 1 - y, ALL, core)
            return [(mine, far, slot, got)]
        if stage == 3:
            mine = view(ALL, ALL, x, core) if self.swap else view(ALL, y, ALL, core)
            got = view(ALL, ALL, x, 1 - core) if self.swap else view(ALL, y, ALL, 1 - core)
        else:
            mine = view(ALL, ALL, 1 - x, core) if self.swap else view(ALL, 1 - y, ALL, core)
            got = view(ALL, ALL, 1 - x, 1 - core) if self.swap else view(ALL, 1 - y, ALL, 1 - core)
        return [(mine, self.core_peer(), slot, got)]

    def start(self, stage):
        for src, target, slot, _ in self.plan(stage):
            self.send(src, src, target, slot)

    def wait(self, stage):
        for _, target, slot, got in self.plan(stage):
            self.copy(got, got, target, slot).wait_recv()


class Scatter(Link):
    def __init__(self, dims, place, given, held, near, far, last, swap, send_sems, recv_sems, base):
        super().__init__(dims, place, send_sems, recv_sems, base)
        self.given, self.held, self.near, self.far, self.last, self.swap = given, held, near, far, last, swap

    def start(self, stage):
        z, y, x, core = self.place
        count = self.dims[0]
        held = self.held
        if stage == 0:
            self.send(self.given(1 - core), held, self.core_peer(), 0)
        elif stage == 1:
            if self.swap:
                self.send(held.at[:, :, 1 - x], self.near, self.x_peer(), 1)
            else:
                self.send(held.at[:, 1 - y], self.near, self.y_peer(), 1)
        elif stage == 2:
            if self.swap:
                self.send(held.at[:, 1 - y, x], self.far, self.y_peer(), 2)
            else:
                self.send(held.at[:, y, 1 - x], self.far, self.x_peer(), 2)
        else:
            for k in range(1, count):
                self.send(held.at[lax.rem(z + k, count), y, x], self.last.at[k - 1], self.z_peer(k), 2 + k)

    def wait(self, stage):
        z, y, x, core = self.place
        count = self.dims[0]
        held = self.held
        if stage == 0:
            self.copy(self.given(1 - core), held, self.core_peer(), 0).wait_recv()
            mine = self.given(core)

            def add(row, carry):
                held[row] = held[row] + mine[row]
                return carry

            lax.fori_loop(0, count, add, 0)
        elif stage == 1:
            self.copy(self.near, self.near, self.core_peer(), 1).wait_recv()

            def add(row, carry):
                if self.swap:
                    held[row, :, x] = held[row, :, x] + self.near[row]
                else:
                    held[row, y] = held[row, y] + self.near[row]
                return carry

            lax.fori_loop(0, count, add, 0)
        elif stage == 2:
            self.copy(self.far, self.far, self.core_peer(), 2).wait_recv()

            def add(row, carry):
                held[row, y, x] = held[row, y, x] + self.far[row]
                return carry

            lax.fori_loop(0, count, add, 0)
        else:
            total = held[z, y, x].astype(jnp.float32)
            for k in range(1, count):
                self.copy(self.last.at[k - 1], self.last.at[k - 1], self.core_peer(), 2 + k).wait_recv()
                total = total + self.last[k - 1].astype(jnp.float32)
            return total


def own_transfers(count, width, rows):
    return count % 8 == 0 and rows * 2 % 8 == 0 and width % 512 == 0


BF16 = jnp.bfloat16
F32 = jnp.float32
LOG2E = 1.4426950408889634
ROWS = 256


def dot(left, right):
    return jnp.dot(left, right, preferred_element_type=F32)


def dot_nt(left, right):
    return lax.dot_general(left, right, (((1,), (1,)), ((), ())), preferred_element_type=F32)


def dot_tn(left, right):
    return lax.dot_general(left, right, (((0,), (0,)), ((), ())), preferred_element_type=F32)


def fold(values):
    return jnp.sum(values.reshape(values.shape[0] // 8, 8, values.shape[1]), axis=0)


def unit(values):
    scale = lax.rsqrt(jnp.mean(values * values, axis=-1, keepdims=True) + norm_eps)
    return values * scale, scale


def unit_back(grad, normal, scale):
    return scale * (grad - normal * jnp.mean(grad * normal, axis=-1, keepdims=True))


def turn_pairs(values, cosine, sine, sign):
    front, back = values[:, : HD // 2], values[:, HD // 2 :]
    if sign > 0:
        return jnp.concatenate([front * cosine - back * sine, back * cosine + front * sine], axis=1)
    return jnp.concatenate([front * cosine + back * sine, back * cosine - front * sine], axis=1)


def column_of(row):
    return jnp.broadcast_to(row, (128, 128)).T


def chunk_masks(per, start, width):
    def owner(count):
        column = lax.broadcasted_iota(jnp.int32, (count, width), 1) + start
        first = lax.broadcasted_iota(jnp.int32, (count, width), 0) * per
        return (column >= first) & (column < first + per)

    entry = lax.broadcasted_iota(jnp.int32, (128, width), 0)
    gap = (lax.broadcasted_iota(jnp.int32, (128, width), 1) + start - entry).astype(F32)
    place = (jnp.floor((gap + 0.5) * (1.0 / per)) * per == gap) & (entry < per)
    return owner, place


def spread_scales(norm_all, rows_ref, scale_ref, per, count):
    flat = norm_all.reshape(count, 8, 128)
    for device in range(count):
        rows_ref[device : device + 1, :] = flat[device, 0:1, :]
    table = rows_ref[...].astype(BF16)
    step = 512

    def part(index, carry):
        start = pl.multiple_of(index * step, step)
        owner, place = chunk_masks(per, start, step)
        spread = dot_tn(table, owner(count).astype(F32).astype(BF16))
        scale_ref[:, pl.ds(start, step)] = jnp.sum(jnp.where(place, spread, 0.0), axis=0, keepdims=True)
        return carry

    lax.fori_loop(0, count * per // step, part, 0)


class Pump:
    RATE = 46500.0
    CORE_RATE = 500000.0
    LATENCY = {"z": 2.8, "x": 1.4, "y": 1.4, "core": 1.0}

    def __init__(self):
        self.now, self.free, self.entries = 0.0, {}, []

    def launch(self, flows):
        done = self.now
        for link, size in flows:
            begin = max(self.now, self.free.get(link, 0.0))
            self.free[link] = begin + size / (self.CORE_RATE if link == "core" else self.RATE)
            done = max(done, self.free[link] + self.LATENCY[link])
        return done

    def add(self, flows, steps):
        entry = [self.launch(flows), 0, steps]
        self.entries.append(entry)
        return entry

    def first(self):
        waiting = [entry for entry in self.entries if entry[1] < len(entry[2])]
        return min(waiting, key=lambda entry: entry[0]) if waiting else None

    def fire(self, entry):
        run, flows = entry[2][entry[1]]
        run()
        self.now = max(self.now, entry[0]) + 0.3
        entry[0] = self.launch(flows)
        entry[1] += 1

    def work(self, time):
        self.now += time
        entry = self.first()
        while entry is not None and entry[0] <= self.now + 0.3:
            self.fire(entry)
            entry = self.first()

    def until(self, target):
        while target[1] < len(target[2]):
            self.fire(self.first())

    def drain(self):
        entry = self.first()
        while entry is not None:
            self.fire(entry)
            entry = self.first()


QKV_CUTS = ((0, 256), (256, 128), (384, 128), (512, 256))


def forward_kernel(dims, x_hbm, cot_hbm, pos_ref, count_ref, freq_ref, qkv_ref, out_ref, gate_up_ref, down_ref, norm_ref,
                   *rest):
    outs, scratch = rest[:25], rest[25:]
    (o_q0, o_q1, o_q2, o_q3, o_wo, o_wgu, o_wd, o_scale, o_normed, o_raw, o_query, o_key, o_value, o_attn, o_cos, o_sin,
     o_ffn_in, o_mid, o_proj, o_hidden, o_gate, o_up, o_ddown, o_out, o_sgrad) = outs
    (q0, q1, q2, q3, wo, wgu, wd, scale, normed, raw, query, key, value, attn_t, cosine, sine,
     ffn_in_t, mid, proj, hidden, gate, up, ddown, out, sgrad,
     x_ref, cot_ref, attn, ffn_in, low, down, norm_all, norm_rows, qkv_got, gate_up_got, pair,
     send_sems, recv_sems, in_sems, out_sems) = scratch
    place = my_place(dims)
    z, y, x, core = place
    count = dims[0] * 8
    tokens = x_ref.shape[0]
    tiles = tokens // ROWS
    loads = [pltpu.make_async_copy(x_hbm, x_ref, in_sems.at[0]), pltpu.make_async_copy(cot_hbm, cot_ref, in_sems.at[1])]
    for load in loads:
        load.start()
    enter(dims, place)
    stores = []

    out_slots = iter(range(48))

    def put(index, part=None):
        src, dst = scratch[index], outs[index]
        if part is not None:
            src, dst = src.at[part], dst.at[part]
        store = pltpu.make_async_copy(src, dst, out_sems.at[next(out_slots)])
        store.start()
        stores.append(store)

    link = Link(dims, place, send_sems, recv_sems, 0)
    for slot, (ref, got) in enumerate(((qkv_ref, qkv_got), (gate_up_ref, gate_up_got))):
        half = got.shape[1]
        other = pl.multiple_of((1 - core) * half, 128)
        link.send(ref.at[:, pl.ds(other, half)], got, link.core_peer(), slot)
    norm_all[z, y, x, core] = jnp.zeros(norm_all.shape[4:], F32)
    norm_all[z, y, x, core, 0:1, 0 : norm_ref.shape[1]] = norm_ref[...].astype(BF16).astype(F32)

    def pair_up(ref, got, slot):
        rows, half = got.shape
        link.copy(got, got, link.core_peer(), slot).wait_recv()
        mine = ref[:, pl.ds(pl.multiple_of(core * half, 128), half)]
        other = got[...]
        first = core == 0
        pair[0:rows, 0:half] = jnp.where(first, mine, other)
        pair[rows : 2 * rows, 0:half] = jnp.where(first, other, mine)

    step = dims[0] + 5
    bases = iter(range(2, 2 + 17 * step, step))

    def item(views):
        return [Gather(dims, place, view, swap == 1, send_sems, recv_sems, next(bases)) for swap, view in enumerate(views)]

    def block(ref, *lead):
        return lambda z, y, x, core: ref.at[(*lead, core, z, y, x)]

    def rows_of(ref, part):
        return lambda z, y, x, core: ref.at[z, y, x, core, part]

    pump = Pump()
    links = [link]

    def gather(parts, sizes):
        links.extend(parts)
        ways = [("x", "y") if not part.swap else ("y", "x") for part in parts]

        def run_near():
            for part in parts:
                part.wait(0)
                part.start(1)

        def run_far():
            for part in parts:
                part.wait(1)
                part.start(2)
                part.start(3)

        def run_core():
            for part in parts:
                part.wait(2)
                part.start(4)

        def run_last():
            for part in parts:
                part.wait(3)
                part.wait(4)

        for part in parts:
            part.start(0)
        near = [(way[0], 4 * size) for way, size in zip(ways, sizes)]
        far = [(way[1], 8 * size) for way, size in zip(ways, sizes)]
        core_flows = [("core", 8 * size) for size in sizes]
        return pump.add(
            [("z", 4 * size) for size in sizes],
            [(run_near, near), (run_far, far + core_flows), (run_core, core_flows), (run_last, [])],
        )

    wo[z, y, x, core] = out_ref[...].astype(BF16).reshape(wo.shape[4:])
    out_entry = gather(item((rows_of(wo, 0), rows_of(wo, 1))), [wo.shape[5] * D * 2] * 2)
    pair_up(qkv_ref, qkv_got, 0)
    for ref, (start, width) in zip((q0, q1, q2, q3), QKV_CUTS):
        ref[core, z, y, x] = pair[:, start : start + width].astype(BF16)
    pump.work(1.5)
    pair_bytes = pair.shape[0] * 2
    sizes = [pair_bytes * width for _, width in QKV_CUTS]
    norm_entry = gather(item((lambda z, y, x, core: norm_all.at[z, y, x, core],)), [4096])
    q_entries = [gather(item((block(q0), block(q1))), sizes[:2]), gather(item((block(q2), block(q3))), sizes[2:])]
    wd[z, y, x, core] = down_ref[...].astype(BF16).reshape(wd.shape[4:])
    down_entry = gather(item((rows_of(wd, 0), rows_of(wd, 1))), [wd.shape[5] * D * 2] * 2)
    pair_up(gate_up_ref, gate_up_got, 1)
    quarters = wgu.shape[0]
    cut = wgu.shape[-1]
    wide_entries = []
    for quarter in range(quarters):
        for colour in range(2):
            start = (2 * quarter + colour) * cut
            wgu[quarter, colour, core, z, y, x] = pair[:, start : start + cut].astype(BF16)
        wide_entries.append(gather(item((block(wgu, quarter, 0), block(wgu, quarter, 1))), [pair_bytes * cut] * 2))
    pump.work(1.0)
    live_tiles = count_ref[0]
    def table_tile(tile, carry):
        span = pl.ds(pl.multiple_of(tile * 128, 128), 128)
        position = column_of(pos_ref[pl.ds(tile, 1), :].astype(F32))
        angle = position * freq_ref[...]
        cosine[span] = jnp.cos(angle)
        sine[span] = jnp.sin(angle)
        row = lax.broadcasted_iota(jnp.int32, (128, 128), 0) + tile * 128
        low[span] = row - jnp.where(tile < live_tiles, jnp.minimum(position.astype(jnp.int32), WIN - 1), 0)
        return carry

    for begin in range(0, tokens // 128, 4):
        lax.fori_loop(begin, begin + 4, table_tile, 0)
        pump.work(1.2)
    put(14)
    put(15)
    for load in loads:
        load.wait()
    pump.until(norm_entry)
    spread_scales(norm_all, norm_rows, scale, norm_ref.shape[1], count)
    put(7)
    pump.work(1.0)
    for entry in q_entries:
        pump.until(entry)
    for index in range(4):
        put(index)

    def scales(which):
        start = (0, D, 2 * D, 3 * D, 4 * D, 4 * D + HD)[which]
        return 1.0 + scale[:, start : start + (D if which < 4 else HD)]

    def weight(ref, c):
        return ref[c].reshape(-1, ref.shape[-1])

    def project(tile, carry):
        rows = pl.ds(pl.multiple_of(tile * ROWS, ROWS), ROWS)
        normal, _ = unit(x_ref[rows].astype(F32))
        inner = (normal * scales(0)).astype(BF16)
        normed[:, rows] = inner.T
        parts = []
        for c in range(2):
            parts.append(dot(inner, weight(q0, c)))
            parts.append(dot(inner, jnp.concatenate([weight(q1, c), weight(q2, c)], axis=1)))
            parts.append(dot(inner, weight(q3, c)))
        for head in range(HQ + 2):
            part = parts[head]
            if head == HQ + 1:
                value[rows] = part.astype(BF16)
                continue
            raw[rows, head * HD : (head + 1) * HD] = part.astype(BF16)
            normal, _ = unit(part)
            turned = turn_pairs(normal * scales(5 if head == HQ else 4), cosine[rows], sine[rows], 1).astype(BF16)
            if head == HQ:
                key[rows] = turned
            else:
                query[rows, head * HD : (head + 1) * HD] = turned
        return carry

    def attend(tile):
        start = tile * ROWS
        rows = slice(start, start + ROWS)
        first = max(0, start - WIN)
        keys = slice(first, start + ROWS)
        lane = lax.broadcasted_iota(jnp.int32, (ROWS, 128), 1)
        row = lax.broadcasted_iota(jnp.int32, (ROWS, 128), 0) + start
        least = low[rows]
        for head in range(HQ):
            span = slice(head * HD, (head + 1) * HD)
            scores = dot_nt(query[rows, span], key[keys])
            parts, total = [], None
            for at in range(first, start + ROWS, 128):
                column = lane + at
                allowed = column >= least
                if at >= start:
                    allowed = allowed & (column <= row)
                part = jnp.where(allowed, jnp.exp2(scores[:, at - first : at - first + 128] * (LOG2E / HD**0.5)), 0.0)
                parts.append(part)
                total = part if total is None else total + part
            inverse = 1.0 / jnp.sum(total, axis=1, keepdims=True)
            probs = jnp.concatenate([(part * inverse).astype(BF16) for part in parts], axis=1)
            attn[rows, span] = dot(probs, value[keys]).astype(BF16)
            attn_t[span, rows] = attn[rows, span].T

    def mix(tile, carry):
        rows = pl.ds(pl.multiple_of(tile * ROWS, ROWS), ROWS)
        projected = dot(attn[rows], wo[...].reshape(-1, D))
        proj[rows] = projected
        normal, _ = unit(projected)
        middle = x_ref[rows].astype(F32) + normal * scales(1)
        mid[rows] = middle
        normal, _ = unit(middle)
        inner = (normal * scales(2)).astype(BF16)
        ffn_in[rows] = inner
        ffn_in_t[:, rows] = inner.T
        return carry

    for begin in range(0, tiles, 2):
        lax.fori_loop(begin, begin + 2, project, 0)
        pump.work(2.6)
    for index in (8, 9, 10, 11, 12):
        put(index)
    for tile in range(tiles):
        attend(tile)
        pump.work(0.5 * min(tile + 1, 3))
    put(13)
    pump.until(out_entry)
    put(4)
    for begin in range(0, tiles, 2):
        lax.fori_loop(begin, begin + 2, mix, 0)
        pump.work(1.8)
    for index in (16, 17, 18):
        put(index)
    pump.until(down_entry)
    put(6)
    wide = 2 * cut
    for quarter in range(quarters):
        pump.until(wide_entries[quarter])

        def feed(tile, carry):
            rows = pl.ds(pl.multiple_of(tile * ROWS, ROWS), ROWS)
            inner = ffn_in[rows]
            total = None
            for colour in range(2):
                at = colour * cut
                gated = dot(inner, weight(wgu.at[quarter, colour], 0))
                upper = dot(inner, weight(wgu.at[quarter, colour], 1))
                square = gated * gated
                bend = jnp.tanh(0.7978845608028654 * (gated + 0.044715 * square * gated))
                half = 0.5 * (1.0 + bend)
                active = gated * half
                slope = half + 0.5 * gated * (1.0 - bend * bend) * (0.7978845608028654 * (1.0 + 0.134145 * square))
                gate[quarter, rows, at : at + cut] = (slope * upper).astype(BF16)
                up[quarter, rows, at : at + cut] = active.astype(BF16)
                inside = (active * upper).astype(BF16)
                first = quarter * wide + at
                hidden[first : first + cut, rows] = inside.T
                part = wd.reshape(FF, D)[first : first + cut, :]
                part = dot(inside, part)
                total = part if total is None else total + part
            if quarter == 0:
                down[rows] = total
            else:
                down[rows] = down[rows] + total
            return carry

        lax.fori_loop(0, tiles, feed, 0)
        pump.work(3.8)
        for index in (5, 20, 21):
            put(index, quarter)
        put(19, pl.ds(quarter * wide, wide))
    sgrad[...] = jnp.zeros_like(sgrad)

    def finish(tile, carry):
        start = pl.multiple_of(tile * ROWS, ROWS)
        rows = pl.ds(start, ROWS)
        normal, factor = unit(down[rows])
        out[rows] = (mid[rows] + normal * scales(3)).astype(BF16)
        row = start + lax.broadcasted_iota(jnp.int32, (ROWS, 1), 0)
        grad = jnp.where(row < live_tiles * TILE, cot_ref[rows].astype(F32), 0.0)
        sgrad[...] += fold(grad * normal)
        ddown[rows] = unit_back(grad * scales(3), normal, factor).astype(BF16)
        return carry

    lax.fori_loop(0, tiles, finish, 0)
    for index in (22, 23, 24):
        put(index)
    pump.drain()
    for each in links:
        each.finish()
    for store in stores:
        store.wait()


def forward_call(dims, block_input, out_cotangent, positions, tile_count, qkv_weight, out_weight, gate_up_weight,
                 down_weight, norm_scales):
    grid = dims[:3]
    tokens = block_input.shape[0]
    rows = qkv_weight.shape[0]
    width, wide = qkv_weight.shape[1], gate_up_weight.shape[1]
    shapes = [((2,) + grid + (2 * rows, cut), BF16) for _, cut in QKV_CUTS] + [
        (grid + (2, 2, out_weight.shape[0] // 2, D), BF16),
        ((4, 2, 2) + grid + (2 * rows, FF // 8), BF16),
        (grid + (2, 2, down_weight.shape[0] // 2, D), BF16),
        ((1, norm_scales.shape[0] * dims[0] * 8), F32),
        ((D, tokens), BF16),
        ((tokens, (HQ + 1) * HD), BF16),
        ((tokens, HQ * HD), BF16),
        ((tokens, HD), BF16),
        ((tokens, HD), BF16),
        ((HQ * HD, tokens), BF16),
        ((tokens, HD // 2), F32),
        ((tokens, HD // 2), F32),
        ((D, tokens), BF16),
        ((tokens, D), F32),
        ((tokens, D), F32),
        ((FF, tokens), BF16),
        ((4, tokens, FF // 4), BF16),
        ((4, tokens, FF // 4), BF16),
        ((tokens, D), BF16),
        ((tokens, D), BF16),
        ((8, D), F32),
    ]
    sems = 2 + 17 * (dims[0] + 5)
    scratch = [pltpu.VMEM(*shape) for shape in shapes] + [
        pltpu.VMEM((tokens, D), BF16),
        pltpu.VMEM((tokens, D), BF16),
        pltpu.VMEM((tokens, HQ * HD), BF16),
        pltpu.VMEM((tokens, D), BF16),
        pltpu.VMEM((tokens, 128), jnp.int32),
        pltpu.VMEM((tokens, D), F32),
        pltpu.VMEM(grid + (2, 8, 128), F32),
        pltpu.VMEM((dims[0] * 8, 128), F32),
        pltpu.VMEM((rows, width // 2), F32),
        pltpu.VMEM((rows, wide // 2), F32),
        pltpu.VMEM((2 * rows, wide // 2), F32),
        pltpu.SemaphoreType.DMA((sems,)),
        pltpu.SemaphoreType.DMA((sems,)),
        pltpu.SemaphoreType.DMA((2,)),
        pltpu.SemaphoreType.DMA((48,)),
    ]
    vmem = pl.BlockSpec(memory_space=pltpu.VMEM)
    hbm = pl.BlockSpec(memory_space=pltpu.HBM)
    frequency = np.power(rope_base, -np.arange(HD // 2) * (2.0 / HD)).astype(np.float32)[None, :]
    return pl.pallas_call(
        functools.partial(forward_kernel, dims),
        out_shape=[jax.ShapeDtypeStruct(*shape) for shape in shapes],
        in_specs=[hbm, hbm, vmem, pl.BlockSpec(memory_space=pltpu.SMEM)] + [vmem] * 6,
        out_specs=[hbm] * len(shapes),
        scratch_shapes=scratch,
        compiler_params=pltpu.CompilerParams(collective_id=0, has_side_effects=True, vmem_limit_bytes=63 << 20),
        name="forward",
    )(block_input, out_cotangent, positions.reshape(-1, 128), tile_count, frequency, qkv_weight, out_weight,
      gate_up_weight, down_weight, norm_scales[None, :])


def backward_kernel(dims, *refs):
    (h_q0, h_q1, h_q2, h_q3, h_wo, h_wgu, h_wd, scale, h_normed, h_raw, h_query, h_key, h_value, h_attn, h_cos, h_sin,
     h_ffn_in, h_mid, h_proj, h_hidden, h_gate, h_up, h_ddown, sgrad_out, h_x, h_cot, pos_ref, count_ref) = refs[:28]
    o_input, o_qkv, o_wo, o_wgu, o_wd, o_norm = refs[28:34]
    (wo, wgu, wd, gq0, gq1, gq2, gq3, go, gg, gd, gn,
     pool, dgu, ddown, ffn_in, attn, dproj, dmid, proj, sine, totals, grow, gtab, bounce, swaps, halves,
     in_sems, out_sem, send_sems, recv_sems) = refs[34:64]
    buffers = list(refs[64:])
    place = my_place(dims)
    z, y, x, core = place
    count = dims[0] * 8
    tokens = dmid.shape[0]
    tiles = tokens // ROWS
    cut = wgu.shape[-1]
    serial = iter(range(64))

    def load(src, dst):
        copy = pltpu.make_async_copy(src, dst, in_sems.at[next(serial)])
        copy.start()
        return copy

    c_ddown = load(h_ddown, ddown)
    c_hidden = [load(h_hidden.at[pl.ds(512 * j, 512)], pool.at[pl.ds(512 * j, 512)]) for j in range(4)]
    c_wd = load(h_wd, wd)
    c_gate = []
    for j in range(4):
        c_gate.append((load(h_gate.at[j], dgu.at[0, j]), load(h_up.at[j], dgu.at[1, j])))
    c_ffn_in = load(h_ffn_in, ffn_in)
    c_wgu = load(h_wgu, wgu)
    c_p3 = [load(h_mid, dmid), load(h_proj, proj), load(h_attn, attn), load(h_wo, wo)]
    enter(dims, place)

    pump = Pump()
    step = dims[0] + 5
    bases = iter(range(12, 12 + 19 * step, step))
    links = []

    def scatter(givens, done):
        parts = []
        for swap, given in enumerate(givens):
            held, near, far, last = buffers[:4]
            del buffers[:4]
            parts.append(Scatter(dims, place, given, held, near, far, last, swap == 1, send_sems, recv_sems, next(bases)))
        links.extend(parts)

        def stage(which):
            def run():
                for part in parts:
                    part.wait(which)
                    part.start(which + 1)

            return run

        def last_stage():
            for colour, part in enumerate(parts):
                done(colour, part.wait(3))

        for part in parts:
            part.start(0)
        sizes = [math.prod(part.last.shape[1:]) * part.last.dtype.itemsize for part in parts]
        ways = [("x", "y") if part.swap else ("y", "x") for part in parts]
        near = [(way[0], 8 * size) for way, size in zip(ways, sizes)]
        far = [(way[1], 4 * size) for way, size in zip(ways, sizes)]
        pump.add(
            [("core", 16 * size) for size in sizes],
            [(stage(0), near), (stage(1), far), (stage(2), [("z", 4 * size) for size in sizes]), (last_stage, [])],
        )

    swap_link = Link(dims, place, send_sems, recv_sems, 0)
    links.append(swap_link)
    fetched = []

    def split_rows(slot, target, start):
        def done(colour, total):
            at = slot + colour
            rows, width = target.shape[0], total.shape[1]
            first = start[colour]
            half = target.shape[1] // 2
            bounce[at % 2, :, 0:width] = total
            low, high = bounce[at % 2, 0:rows, 0:width], bounce[at % 2, rows : 2 * rows, 0:width]
            target[:, pl.ds(pl.multiple_of(core * half + first, 128), width)] = jnp.where(core == 0, low, high)
            swaps[at, :, 0:width] = jnp.where(core == 0, high, low)
            span = (at, slice(None), pl.ds(0, width))
            swap_link.send(swaps.at[span], halves.at[span], swap_link.core_peer(), at)

            def fetch():
                swap_link.copy(halves.at[span], halves.at[span], swap_link.core_peer(), at).wait_recv()
                target[:, pl.ds(pl.multiple_of((1 - core) * half + first, 128), width)] = halves[at, :, 0:width]

            fetched.append(fetch)

        return done

    def rows_done(target, start):
        def done(colour, total):
            height = total.shape[0]
            first = start + colour * height
            target[first : first + height, :] = total

        return done

    def scales(which):
        start = (0, D, 2 * D, 3 * D, 4 * D, 4 * D + HD)[which]
        return 1.0 + scale[:, start : start + (D if which < 4 else HD)]

    def weight(ref, c):
        return ref[c].reshape(-1, ref.shape[-1])

    def some_rows(tile):
        return pl.ds(pl.multiple_of(tile * ROWS, ROWS), ROWS)

    c_ddown.wait()
    grown = gd.reshape(FF, D)
    for copy in c_hidden:
        copy.wait()

    def down_part(part, carry):
        rows = pl.ds(pl.multiple_of(part * 512, 512), 512)
        grown[rows, :] = dot(pool[rows, :], ddown[...]).astype(BF16)
        return carry

    lax.fori_loop(0, FF // 512, down_part, 0)
    for sub in range(2):
        scatter([(lambda core, k=2 * sub + k: gd.at[:, :, :, core, k]) for k in range(2)],
                rows_done(o_wd, sub * 2 * gd.shape[5]))
    queries, others = pool.at[pl.ds(0, tokens)], pool.at[pl.ds(tokens, tokens)]
    c_query = [load(h_query, queries), load(h_key, others.at[:, pl.ds(0, HD)]), load(h_value, others.at[:, pl.ds(HD, HD)])]
    c_wd.wait()
    c_ffn_in.wait()
    down_rows = wd.reshape(FF, D)
    for quarter in range(4):
        for copy in c_gate[quarter]:
            copy.wait()
        last_rows = slice(quarter * 512, (quarter + 1) * 512)

        def spread(tile, carry, quarter=quarter, last_rows=last_rows):
            rows = some_rows(tile)
            grad = dot_nt(ddown[rows], down_rows[last_rows, :])
            dgu[0, quarter, rows] = (grad * dgu[0, quarter, rows].astype(F32)).astype(BF16)
            dgu[1, quarter, rows] = (grad * dgu[1, quarter, rows].astype(F32)).astype(BF16)
            return carry

        lax.fori_loop(0, tiles, spread, 0)
        pump.work(1.2)

        def wide_part(c, carry, quarter=quarter):
            for colour in range(2):
                span = slice(colour * cut, (colour + 1) * cut)
                gg[quarter, colour, c] = dot(ffn_in[...], dgu[c, quarter, :, span]).astype(BF16).reshape(gg.shape[3:])
            return carry

        lax.fori_loop(0, 2, wide_part, 0)
        pump.work(1.8)
        scatter([(lambda core, q=quarter, k=k: gg.at[q, k, core]) for k in range(2)],
                split_rows(2 * quarter, o_wgu, [(2 * quarter + k) * cut for k in range(2)]))
        pump.work(0.1)
    xc = ddown
    c_p3.append(load(h_cot, xc))
    c_normed = load(h_normed, ffn_in)
    c_wgu.wait()
    for copy in c_p3:
        copy.wait()
    names = ("in", "post", "ffn", "out", "query", "key")
    sums = dict(zip(names, (slice(8 * index, 8 * index + 8) for index in range(6))))
    totals[...] = jnp.zeros_like(totals)

    def collect(which, values):
        totals[sums[which], 0 : values.shape[1]] += fold(values)

    def middle_tile(tile, carry):
        rows = some_rows(tile)
        grad = None
        for quarter in range(4):
            for c in range(2):
                part = jnp.concatenate([weight(wgu.at[quarter, colour], c) for colour in range(2)], axis=1)
                part = dot_nt(dgu[c, quarter, rows], part)
                grad = part if grad is None else grad + part
        row = tile * ROWS + lax.broadcasted_iota(jnp.int32, (ROWS, 1), 0)
        given = jnp.where(row < count_ref[0] * TILE, xc[rows].astype(F32), 0.0)
        normal, factor = unit(dmid[rows])
        collect("ffn", grad * normal)
        middle = given + unit_back(grad * scales(2), normal, factor)
        dmid[rows] = middle
        normal, factor = unit(proj[rows])
        collect("post", middle * normal)
        dproj[rows] = unit_back(middle * scales(1), normal, factor).astype(BF16)
        return carry

    for begin in range(0, tiles, 2):
        lax.fori_loop(begin, begin + 2, middle_tile, 0)
        pump.work(4.4)
    c_raw = [load(h_raw.at[:, pl.ds(0, 512)], dgu.at[0, 0]), load(h_raw.at[:, pl.ds(512, 512)], dgu.at[0, 1]),
             load(h_raw.at[:, pl.ds(1024, HD)], dgu.at[0, 2, :, pl.ds(0, HD)])]
    cosine = proj.at[:, pl.ds(2 * HD, HD // 2)]
    c_rest = [load(h_cos, cosine), load(h_sin, sine), load(h_x, xc)]
    wq = wd.reshape(FF, D)
    c_qkv = []
    for c in range(2):
        for ref, within, lane in ((h_q0, 0, 0), (h_q1, 1, 0), (h_q2, 1, 128), (h_q3, 2, 0)):
            head = 3 * c + within
            at = pl.ds(head % 2 * HD + lane, ref.shape[-1])
            c_qkv.append(load(ref.at[c], wq.at[pl.ds(head // 2 * D, D), at]))
    grown_out = go.reshape(HQ * HD, D)
    for half in range(2):
        rows = slice(half * 512, (half + 1) * 512)
        grown_out[rows, :] = dot(attn[rows, :], dproj[...]).astype(BF16)
    scatter([(lambda core, k=k: go.at[:, :, :, core, k]) for k in range(2)], rows_done(o_wo, 0))
    out_rows = wo.reshape(HQ * HD, D)
    pump.work(1.9)

    def attn_grad(tile, carry):
        rows = some_rows(tile)
        attn[rows] = dot_nt(dproj[rows], out_rows[...]).astype(BF16)
        return carry

    lax.fori_loop(0, tiles, attn_grad, 0)
    pump.work(1.9)
    for copy in c_query + c_raw + c_rest:
        copy.wait()
    dkey, dvalue = proj.at[:, pl.ds(0, HD)], proj.at[:, pl.ds(HD, HD)]

    for tile in range(tiles):
        start = tile * ROWS
        rows = slice(start, start + ROWS)
        first = max(0, start - WIN)
        keys = slice(first, start + ROWS)
        height = start + ROWS - first
        position = jnp.concatenate([pos_ref[2 * tile : 2 * tile + 1, :], pos_ref[2 * tile + 1 : 2 * tile + 2, :]], axis=1)
        row = lax.broadcasted_iota(jnp.int32, (1, ROWS), 1) + start
        reach = jnp.where(row < count_ref[0] * TILE, jnp.minimum(position, WIN - 1), 0)
        column = lax.broadcasted_iota(jnp.int32, (height, ROWS), 0) + first
        allowed = (column >= row - reach) & (column <= row)
        dvalue[rows, :] = jnp.zeros((ROWS, HD), F32)
        dkey[rows, :] = jnp.zeros((ROWS, HD), F32)

        def two_heads(pair, carry, rows=rows, keys=keys, allowed=allowed):
            key, value = others[keys, 0:HD], others[keys, HD : 2 * HD]
            probs_all, scores_all, query_all, grads_all = [], [], [], []
            for each in range(2):
                span = pl.ds(pl.multiple_of((2 * pair + each) * HD, HD), HD)
                query = queries[rows, span]
                grad = attn[rows, span]
                weights = jnp.where(allowed, jnp.exp2(dot_nt(key, query) * (LOG2E / HD**0.5)), 0.0)
                probs = weights * (1.0 / jnp.sum(weights, axis=0, keepdims=True))
                grad_probs = dot_nt(value, grad)
                both = probs * grad_probs
                delta = jnp.sum(both, axis=0, keepdims=True)
                scores = ((both - probs * delta) * HD**-0.5).astype(BF16)
                probs_all.append(probs.astype(BF16))
                scores_all.append(scores)
                query_all.append(query)
                grads_all.append(grad)
            dvalue[keys, :] += dot(jnp.concatenate(probs_all, axis=1), jnp.concatenate(grads_all, axis=0))
            dkey[keys, :] += dot(jnp.concatenate(scores_all, axis=1), jnp.concatenate(query_all, axis=0))
            for each in range(2):
                span = pl.ds(pl.multiple_of((2 * pair + each) * HD, HD), HD)
                grad = turn_pairs(dot_tn(scores_all[each], key), cosine[rows, :], sine[rows, :], -1)
                normal, factor = unit(dgu[0, pair, rows, each * HD : (each + 1) * HD].astype(F32))
                collect("query", grad * normal)
                queries[rows, span] = unit_back(grad * scales(4), normal, factor).astype(BF16)
            return carry

        lax.fori_loop(0, HQ // 2, two_heads, 0)
        pump.work((1.3, 2.3, 3.3, 3.3)[min(tile, 3)])

    def key_tile(tile, carry):
        rows = some_rows(tile)
        grad = turn_pairs(dkey[rows, :], cosine[rows, :], sine[rows, :], -1)
        normal, factor = unit(dgu[0, 2, rows, 0:HD].astype(F32))
        collect("key", grad * normal)
        others[rows, 2 * HD : 3 * HD] = unit_back(grad * scales(5), normal, factor).astype(BF16)
        others[rows, 3 * HD : 4 * HD] = dvalue[rows, :].astype(BF16)
        return carry

    lax.fori_loop(0, tiles, key_tile, 0)
    pump.work(1.0)
    c_normed.wait()

    def grad_columns(rows, head):
        ref, at = (queries, head * HD) if head < HQ else (others, (head - HQ + 2) * HD)
        return ref[rows, at : at + HD]

    for head in range(HQ + 2):
        term = dot(ffn_in[...], grad_columns(slice(0, tokens), head)).astype(BF16)
        c, within = head // 3, head % 3
        if within == 0:
            gq0[c] = term.reshape(gq0.shape[1:])
        elif within == 2:
            gq3[c] = term.reshape(gq3.shape[1:])
        else:
            gq1[c] = term[:, 0:128].reshape(gq1.shape[1:])
            gq2[c] = term[:, 128:256].reshape(gq2.shape[1:])
    for sub, pair in enumerate(((gq0, gq1), (gq2, gq3))):
        scatter([(lambda core, ref=ref: ref.at[core]) for ref in pair],
                split_rows(8 + 2 * sub, o_qkv, [QKV_CUTS[2 * sub + k][0] for k in range(2)]))
    pump.work(2.8)
    for copy in c_qkv:
        copy.wait()

    def input_tile(tile, carry):
        rows = some_rows(tile)
        grad = None
        for head in range(HQ + 2):
            part = wq[head // 2 * D : (head // 2 + 1) * D, head % 2 * HD : (head % 2 + 1) * HD]
            part = dot_nt(grad_columns(rows, head), part)
            grad = part if grad is None else grad + part
        normal, factor = unit(xc[rows].astype(F32))
        collect("in", grad * normal)
        dmid[rows] = dmid[rows] + unit_back(grad * scales(0), normal, factor)
        return carry

    lax.fori_loop(0, tiles, input_tile, 0)
    pump.work(4.4)
    store = pltpu.make_async_copy(dmid, o_input, out_sem)
    store.start()
    totals[sums["out"]] = sgrad_out[...]
    at = 0
    for index, name in enumerate(names):
        size = D if index < 4 else HD
        grow[:, at : at + size] = jnp.sum(totals[sums[name], 0:size], axis=0, keepdims=True)
        at += size
    per = at // count

    def chunk_part(index, table):
        begin = pl.multiple_of(index * 512, 512)
        owner, entry = chunk_masks(per, begin, 512)
        picked = entry.astype(F32).astype(BF16)
        rest = jnp.where(owner(count), grow[:, pl.ds(begin, 512)], 0.0)
        for _ in range(3):
            piece = rest.astype(BF16)
            rest = rest - piece.astype(F32)
            table = table + dot_nt(piece, picked)
        return table

    gtab[...] = lax.fori_loop(0, at // 512, chunk_part, jnp.zeros((count, 128), F32))
    flat = gn.reshape(count, 8, 128)
    for device in range(count):
        flat[device] = jnp.broadcast_to(gtab[device : device + 1, :], (8, 128))

    def norm_done(colour, total):
        o_norm[...] = total

    scatter([lambda core: gn.at[:, :, :, core]], norm_done)
    pump.drain()
    for fetch in fetched:
        fetch()
    for link in links:
        link.finish()
    store.wait()


def backward_call(dims, saved, block_input, out_cotangent, positions, tile_count, shard_rows):
    grid = dims[:3]
    count = dims[0] * 8
    tokens = block_input.shape[0]
    qkv_rows, out_rows, down_rows, norm_rows = shard_rows
    width = (HQ + 2) * HD
    bf = lambda *shape: pltpu.VMEM(shape, BF16)
    fp = lambda *shape: pltpu.VMEM(shape, F32)
    pair = 2 * qkv_rows
    weights = [bf(*((2,) + grid + (pair, cut))) for _, cut in QKV_CUTS] + [
        bf(*(grid + (2, 2, out_rows // 2, D))),
        bf(*((4, 2, 2) + grid + (pair, FF // 8))),
        bf(*(grid + (2, 2, down_rows // 2, D))),
    ]
    scratch = weights[4:] + weights[:6] + [
        bf(*(grid + (2, 4, down_rows // 4, D))),
        fp(*(grid + (2, 8, 128))),
        bf(FF, tokens),
        bf(2, 4, tokens, FF // 4),
        bf(tokens, D),
        bf(D, tokens),
        bf(HQ * HD, tokens),
        bf(tokens, D),
        fp(tokens, D),
        fp(tokens, D),
        fp(tokens, HD // 2),
        fp(48, D),
        fp(1, 4 * D + 2 * HD),
        fp(count, 128),
        fp(2, pair, 256),
        fp(12, qkv_rows, 256),
        fp(12, qkv_rows, 256),
        pltpu.SemaphoreType.DMA((64,)),
        pltpu.SemaphoreType.DMA,
    ]
    sems = 12 + 19 * (dims[0] + 5)
    scratch += [pltpu.SemaphoreType.DMA((sems,)), pltpu.SemaphoreType.DMA((sems,))]
    blocks = [[(down_rows // 4, D)] * 2] * 2 + [[(pair, FF // 8)] * 2] * 4 + [[(out_rows // 2, D)] * 2]
    blocks += [[(pair, QKV_CUTS[0][1]), (pair, QKV_CUTS[1][1])], [(pair, QKV_CUTS[2][1]), (pair, QKV_CUTS[3][1])], [(8, 128)]]
    for colours in blocks:
        for swap, block in enumerate(colours):
            make = fp if block == (8, 128) else bf
            scratch.append(make(*(grid + block)))
            scratch.append(make(*(((grid[0], grid[1]) if swap else (grid[0], grid[2])) + block)))
            scratch.append(make(*((grid[0],) + block)))
            scratch.append(make(*((grid[0] - 1,) + block)))
    vmem = pl.BlockSpec(memory_space=pltpu.VMEM)
    hbm = pl.BlockSpec(memory_space=pltpu.HBM)
    outs = [(tokens, D), (qkv_rows, width), (out_rows, D), (qkv_rows, 2 * FF), (down_rows, D), (8, 128)]
    saved = list(saved)
    saved[:4] = [array.reshape(2, D, -1) for array in saved[:4]]
    inputs = saved[:23] + [saved[24], block_input, out_cotangent, positions.reshape(-1, 128), tile_count]
    specs = [hbm] * 28
    specs[7] = specs[23] = specs[26] = vmem
    specs[27] = pl.BlockSpec(memory_space=pltpu.SMEM)
    return pl.pallas_call(
        functools.partial(backward_kernel, dims),
        out_shape=[jax.ShapeDtypeStruct(shape, F32) for shape in outs],
        in_specs=specs,
        out_specs=[hbm] + [vmem] * 5,
        scratch_shapes=scratch,
        compiler_params=pltpu.CompilerParams(collective_id=1, has_side_effects=True, vmem_limit_bytes=67043328),
        name="backward",
    )(*inputs)


def adam_kernel(*refs):
    ins, outs, bufs = refs[:22], refs[22:44], refs[44:66]
    in_sems, out_sems = refs[66:]
    loads = [pltpu.make_async_copy(src, buf, in_sems.at[at]) for at, (src, buf) in enumerate(zip(ins, bufs))]
    stores = [pltpu.make_async_copy(buf, dst, out_sems.at[at]) for at, (buf, dst) in enumerate(zip(bufs, outs))]
    for load in loads:
        load.start()
    for item in range(5):
        span = range(4 * item, 4 * item + 4)
        for at in span:
            loads[at].wait()
        stores[4 * item].start()
        grad, weight, first, second = (bufs[at] for at in span)
        size = weight.shape[1]
        news = adam_update(weight[...], grad[0 : weight.shape[0], 0:size], first[...], second[...])
        for ref, new in zip((weight, first, second), news):
            ref[...] = new
        for at in span[1:]:
            stores[at].start()
    for at in (20, 21):
        loads[at].wait()
        stores[at].start()
    for store in stores:
        store.wait()


def adam_call(groups, passed):
    flat = [array if array.ndim == 2 else array[None, :] for group in groups for array in group] + list(passed)
    hbm = pl.BlockSpec(memory_space=pltpu.HBM)
    outs = pl.pallas_call(
        adam_kernel,
        out_shape=[jax.ShapeDtypeStruct(array.shape, array.dtype) for array in flat],
        in_specs=[hbm] * 22,
        out_specs=[hbm] * 22,
        scratch_shapes=[pltpu.VMEM(array.shape, array.dtype) for array in flat]
        + [pltpu.SemaphoreType.DMA((22,)), pltpu.SemaphoreType.DMA((22,))],
        compiler_params=pltpu.CompilerParams(vmem_limit_bytes=67043328),
        name="adam",
    )(*flat)
    results = []
    for item, group in enumerate(groups):
        shape = group[1].shape
        part = list(outs[4 * item : 4 * item + 4])
        if part[0].shape != part[1].shape:
            part[0] = part[0][0, : shape[0]]
        results.append([array.reshape(shape) for array in part])
    return results, outs[20:]


def plain_pass(
    block_input,
    out_cotangent,
    segment_ids,
    positions,
    tile_count,
    qkv_weight,
    out_weight,
    gate_up_weight,
    down_weight,
    norm_scales,
):
    qkv_full, out_full, gate_up_full, down_full, norm_full = (
        lax.all_gather(array.astype(jnp.bfloat16), "dp", axis=0, tiled=True)
        for array in (qkv_weight, out_weight, gate_up_weight, down_weight, norm_scales)
    )
    attn_full = (qkv_full, out_full, norm_full)
    ffn_full = (gate_up_full, down_full)
    row_count = block_input.shape[0]
    live_rows = jnp.arange(row_count, dtype=jnp.int32) // TILE < tile_count[0]
    block_output, attn_saved, ffn_saved = forward_pass(
        attn_full, ffn_full, block_input, segment_ids, positions, live_rows
    )
    attn_back, ffn_back = attn_full, ffn_full
    grad_out = out_cotangent.astype(jnp.float32) * live_rows[:, None].astype(jnp.float32)
    d_mid, gate_up_term, down_term, ffn_scale_grad, out_scale_grad = ffn_backward(
        ffn_back, attn_back[2].astype(jnp.float32), ffn_saved, grad_out
    )
    (
        input_grad,
        qkv_term,
        out_term,
        in_scale_grad,
        post_scale_grad,
        query_scale_grad,
        key_scale_grad,
    ) = attn_backward(attn_back, attn_saved, d_mid)
    norm_term = jnp.concatenate(
        [
            in_scale_grad,
            post_scale_grad,
            ffn_scale_grad,
            out_scale_grad,
            query_scale_grad,
            key_scale_grad,
        ]
    )
    sums = tuple(
        lax.psum_scatter(term, "dp", scatter_dimension=0, tiled=True)
        for term in (qkv_term, out_term, gate_up_term, down_term, norm_term)
    )
    return (block_output, input_grad) + sums


def shards(
    count,
    block_input,
    out_cotangent,
    segment_ids,
    positions,
    tile_count,
    qkv_weight,
    qkv_first,
    qkv_second,
    out_weight,
    out_first,
    out_second,
    gate_up_weight,
    gate_up_first,
    gate_up_second,
    down_weight,
    down_first,
    down_second,
    norm_scales,
    norm_first,
    norm_second,
):
    dims = grid_dims(count)
    if own_transfers(count, qkv_weight.shape[1], qkv_weight.shape[0]):
        saved = forward_call(
            dims, block_input, out_cotangent, positions, tile_count, qkv_weight, out_weight, gate_up_weight, down_weight,
            norm_scales,
        )
        block_output = saved[23]
        shard_rows = (qkv_weight.shape[0], out_weight.shape[0], down_weight.shape[0], norm_scales.shape[0])
        input_grad, qkv_grad, out_grad, gate_up_grad, down_grad, norm_grad = backward_call(
            dims, saved, block_input, out_cotangent, positions, tile_count, shard_rows
        )
    else:
        block_output, input_grad, qkv_grad, out_grad, gate_up_grad, down_grad, norm_grad = plain_pass(
            block_input, out_cotangent, segment_ids, positions, tile_count, qkv_weight, out_weight, gate_up_weight,
            down_weight, norm_scales,
        )
    (
        (
            (qkv_grad, qkv_new, qkv_first_new, qkv_second_new),
            (out_grad, out_new, out_first_new, out_second_new),
            (gate_up_grad, gate_up_new, gate_up_first_new, gate_up_second_new),
            (down_grad, down_new, down_first_new, down_second_new),
            (norm_grad, norms_new, norm_first_new, norm_second_new),
        ),
        (block_output, input_grad),
    ) = adam_call(
        (
            (qkv_grad, qkv_weight, qkv_first, qkv_second),
            (out_grad, out_weight, out_first, out_second),
            (gate_up_grad, gate_up_weight, gate_up_first, gate_up_second),
            (down_grad, down_weight, down_first, down_second),
            (norm_grad, norm_scales, norm_first, norm_second),
        ),
        (block_output, input_grad),
    )
    return (
        block_output,
        input_grad,
        qkv_grad,
        out_grad,
        gate_up_grad,
        down_grad,
        norm_grad,
        qkv_new,
        out_new,
        gate_up_new,
        down_new,
        norms_new,
        qkv_first_new,
        out_first_new,
        gate_up_first_new,
        down_first_new,
        norm_first_new,
        qkv_second_new,
        out_second_new,
        gate_up_second_new,
        down_second_new,
        norm_second_new,
    )


def solution(mesh):
    in_specs = (
        P("dp", None),
        P("dp", None),
        P("dp"),
        P("dp"),
        P("dp"),
        P("dp", None),
        P("dp", None),
        P("dp", None),
        P("dp", None),
        P("dp", None),
        P("dp", None),
        P("dp", None),
        P("dp", None),
        P("dp", None),
        P("dp", None),
        P("dp", None),
        P("dp", None),
        P("dp"),
        P("dp"),
        P("dp"),
    )
    out_specs = (
        P("dp", None),
        P("dp", None),
        P("dp", None),
        P("dp", None),
        P("dp", None),
        P("dp", None),
        P("dp"),
        P("dp", None),
        P("dp", None),
        P("dp", None),
        P("dp", None),
        P("dp"),
        P("dp", None),
        P("dp", None),
        P("dp", None),
        P("dp", None),
        P("dp"),
        P("dp", None),
        P("dp", None),
        P("dp", None),
        P("dp", None),
        P("dp"),
    )
    body = functools.partial(shards, mesh.shape["dp"])
    return jax.shard_map(body, mesh=mesh, in_specs=in_specs, out_specs=out_specs, check_vma=False)
```

profile of v0, /device:TPU:0, one launch (start us, length us, event | category | flops | bytes accessed | tf_op | source)
XLA Modules:
  0.0 169.4 jit_solution(14411097474876002710)
XLA Ops:
  1.3 79.7 %forward.1 = (bf16[2,4,2,2,40,256]{5,4,3,2,1,0:T(8,128)(2,1)}, bf16[2,4,2,2,40,128]{5,4,3,2,1,0:T(8,128)(2,1)}, bf16[2,4,2,2,40,128]{5,4,3,2,1,0:T(8,128)(2,1)},...) custom-call(bf16[1024,640]{1,0:T(8,128)(2,1)} %refs_24_.1, ...), custom_call_target="tpu_custom_call" | custom-call | tf_op jit(solution)/shard_map/forward/pallas_call | solution.py:953
  81.1 80.3 %backward.1 = (f32[1024,640]{1,0:T(8,128)}, f32[20,1536]{1,0:T(8,128)}, f32[32,640]{1,0:T(8,128)}, f32[20,4096]{1,0:T(8,128)}, f32[64,640]{1,0:T(8,128)}, /*index=5*/f32[8,128]{1,0:T(8,128)}) custom-call(bf16[2,640,256]{2,1,0:T(8,128)(2,1)} %bitcast.13, bf16[2,640,128]{2,1,0:T(8,128)(2,1)} %bitcast.15, bf16[2,640,128]{2,1,0:T(8,128)(2,1)} %bitcast.16, ...), custom_call_target="tpu_custom_call" | custom-call | tf_op jit(solution)/shard_map/backward/pallas_call | solution.py:1371
  161.4 6.8 %adam.1 = (f32[20,1536]{1,0:T(8,128)}, f32[20,1536]{1,0:T(8,128)}, f32[20,1536]{1,0:T(8,128)}, f32[20,1536]{1,0:T(8,128)}, f32[32,640]{1,0:T(8,128)}, /*index=5*...) custom-call(f32[20,1536]{1,0:T(8,128)} %get-tuple-element.99.refs_0_, ...), custom_call_target="tpu_custom_call" | custom-call | tf_op jit(solution)/shard_map/adam/pallas_call | solution.py:1411
  168.2 1.2 slice_bitcast_fusion
where the time goes:
time: 170 us; the launch traced here: 169 us
  Pallas kernels  167 us (98%)
    pallas_call x1, Pallas kernels, backward_call(): pl.pallas_call(functools.partial(backward_kernel, dims), out_shape=[jax.S...  80.3 us
    pallas_call x1, Pallas kernels, forward_call(): pl.pallas_call(functools.partial(forward_kernel, dims), out_shape=[jax.Sh...  79.7 us
    pallas_call x1, Pallas kernels, adam_call(): pl.pallas_call(adam_kernel, out_shape=[jax.ShapeDtypeStruct(array.shape,...  6.82 us

commit v1 on v0

--- a/solution.py
+++ b/solution.py
@@ -608,24 +608,27 @@
 QKV_CUTS = ((0, 256), (256, 128), (384, 128), (512, 256))
 
 
-def forward_kernel(dims, x_hbm, cot_hbm, pos_ref, count_ref, freq_ref, qkv_ref, out_ref, gate_up_ref, down_ref, norm_ref,
-                   *rest):
+def forward_kernel(dims, x_hbm, cot_hbm, pos_ref, count_ref, freq_ref, qkv_hbm, out_hbm, gate_up_hbm, down_hbm,
+                   norm_ref, *rest):
     outs, scratch = rest[:25], rest[25:]
     (o_q0, o_q1, o_q2, o_q3, o_wo, o_wgu, o_wd, o_scale, o_normed, o_raw, o_query, o_key, o_value, o_attn, o_cos, o_sin,
      o_ffn_in, o_mid, o_proj, o_hidden, o_gate, o_up, o_ddown, o_out, o_sgrad) = outs
     (q0, q1, q2, q3, wo, wgu, wd, scale, normed, raw, query, key, value, attn_t, cosine, sine,
      ffn_in_t, mid, proj, hidden, gate, up, ddown, out, sgrad,
-     x_ref, cot_ref, attn, ffn_in, low, down, norm_all, norm_rows, qkv_got, gate_up_got, pair,
+     x_ref, cot_ref, qkv_ref, out_ref, gate_up_ref, down_ref, attn, ffn_in, low, down, norm_all, norm_rows, qkv_got, gate_up_got, pair,
      send_sems, recv_sems, in_sems, out_sems) = scratch
     place = my_place(dims)
     z, y, x, core = place
     count = dims[0] * 8
     tokens = x_ref.shape[0]
     tiles = tokens // ROWS
-    loads = [pltpu.make_async_copy(x_hbm, x_ref, in_sems.at[0]), pltpu.make_async_copy(cot_hbm, cot_ref, in_sems.at[1])]
+    sources = ((qkv_hbm, qkv_ref), (out_hbm, out_ref), (gate_up_hbm, gate_up_ref), (down_hbm, down_ref), (x_hbm, x_ref), (cot_hbm, cot_ref))
+    loads = [pltpu.make_async_copy(src, dst, in_sems.at[at]) for at, (src, dst) in enumerate(sources)]
     for load in loads:
         load.start()
     enter(dims, place)
+    for load in loads[:4]:
+        load.wait()
     stores = []
 
     out_slots = iter(range(48))
@@ -743,7 +746,7 @@
         pump.work(1.2)
     put(14)
     put(15)
-    for load in loads:
+    for load in loads[4:]:
         load.wait()
     pump.until(norm_entry)
     spread_scales(norm_all, norm_rows, scale, norm_ref.shape[1], count)
@@ -842,11 +845,22 @@
     pump.until(down_entry)
     put(6)
     wide = 2 * cut
+    sgrad[...] = jnp.zeros_like(sgrad)
+
+    def finish(rows, start, total):
+        normal, factor = unit(total)
+        out[rows] = (mid[rows] + normal * scales(3)).astype(BF16)
+        row = start + lax.broadcasted_iota(jnp.int32, (ROWS, 1), 0)
+        grad = jnp.where(row < live_tiles * TILE, cot_ref[rows].astype(F32), 0.0)
+        sgrad[...] += fold(grad * normal)
+        ddown[rows] = unit_back(grad * scales(3), normal, factor).astype(BF16)
+
     for quarter in range(quarters):
         pump.until(wide_entries[quarter])
 
         def feed(tile, carry):
-            rows = pl.ds(pl.multiple_of(tile * ROWS, ROWS), ROWS)
+            begin = pl.multiple_of(tile * ROWS, ROWS)
+            rows = pl.ds(begin, ROWS)
             inner = ffn_in[rows]
             total = None
             for colour in range(2):
@@ -868,8 +882,10 @@
                 total = part if total is None else total + part
             if quarter == 0:
                 down[rows] = total
+            elif quarter < quarters - 1:
+                down[rows] = down[rows] + total
             else:
-                down[rows] = down[rows] + total
+                finish(rows, begin, down[rows] + total)
             return carry
 
         lax.fori_loop(0, tiles, feed, 0)
@@ -877,20 +893,6 @@
         for index in (5, 20, 21):
             put(index, quarter)
         put(19, pl.ds(quarter * wide, wide))
-    sgrad[...] = jnp.zeros_like(sgrad)
-
-    def finish(tile, carry):
-        start = pl.multiple_of(tile * ROWS, ROWS)
-        rows = pl.ds(start, ROWS)
-        normal, factor = unit(down[rows])
-        out[rows] = (mid[rows] + normal * scales(3)).astype(BF16)
-        row = start + lax.broadcasted_iota(jnp.int32, (ROWS, 1), 0)
-        grad = jnp.where(row < live_tiles * TILE, cot_ref[rows].astype(F32), 0.0)
-        sgrad[...] += fold(grad * normal)
-        ddown[rows] = unit_back(grad * scales(3), normal, factor).astype(BF16)
-        return carry
-
-    lax.fori_loop(0, tiles, finish, 0)
     for index in (22, 23, 24):
         put(index)
     pump.drain()
@@ -933,6 +935,10 @@
     scratch = [pltpu.VMEM(*shape) for shape in shapes] + [
         pltpu.VMEM((tokens, D), BF16),
         pltpu.VMEM((tokens, D), BF16),
+        pltpu.VMEM(qkv_weight.shape, F32),
+        pltpu.VMEM(out_weight.shape, F32),
+        pltpu.VMEM(gate_up_weight.shape, F32),
+        pltpu.VMEM(down_weight.shape, F32),
         pltpu.VMEM((tokens, HQ * HD), BF16),
         pltpu.VMEM((tokens, D), BF16),
         pltpu.VMEM((tokens, 128), jnp.int32),
@@ -944,7 +950,7 @@
         pltpu.VMEM((2 * rows, wide // 2), F32),
         pltpu.SemaphoreType.DMA((sems,)),
         pltpu.SemaphoreType.DMA((sems,)),
-        pltpu.SemaphoreType.DMA((2,)),
+        pltpu.SemaphoreType.DMA((6,)),
         pltpu.SemaphoreType.DMA((48,)),
     ]
     vmem = pl.BlockSpec(memory_space=pltpu.VMEM)
@@ -953,7 +959,7 @@
     return pl.pallas_call(
         functools.partial(forward_kernel, dims),
         out_shape=[jax.ShapeDtypeStruct(*shape) for shape in shapes],
-        in_specs=[hbm, hbm, vmem, pl.BlockSpec(memory_space=pltpu.SMEM)] + [vmem] * 6,
+        in_specs=[hbm, hbm, vmem, pl.BlockSpec(memory_space=pltpu.SMEM), vmem] + [hbm] * 4 + [vmem],
         out_specs=[hbm] * len(shapes),
         scratch_shapes=scratch,
         compiler_params=pltpu.CompilerParams(collective_id=0, has_side_effects=True, vmem_limit_bytes=63 << 20),
@@ -986,12 +992,9 @@
     c_ddown = load(h_ddown, ddown)
     c_hidden = [load(h_hidden.at[pl.ds(512 * j, 512)], pool.at[pl.ds(512 * j, 512)]) for j in range(4)]
     c_wd = load(h_wd, wd)
-    c_gate = []
-    for j in range(4):
-        c_gate.append((load(h_gate.at[j], dgu.at[0, j]), load(h_up.at[j], dgu.at[1, j])))
+    c_gate = [(load(h_gate.at[j], dgu.at[0, j]), load(h_up.at[j], dgu.at[1, j])) for j in range(4)]
     c_ffn_in = load(h_ffn_in, ffn_in)
-    c_wgu = load(h_wgu, wgu)
-    c_p3 = [load(h_mid, dmid), load(h_proj, proj), load(h_attn, attn), load(h_wo, wo)]
+    c_p3 = [load(h_wgu, wgu), load(h_mid, dmid), load(h_proj, proj), load(h_attn, attn), load(h_wo, wo)]
     enter(dims, place)
 
     pump = Pump()
@@ -1121,7 +1124,6 @@
     xc = ddown
     c_p3.append(load(h_cot, xc))
     c_normed = load(h_normed, ffn_in)
-    c_wgu.wait()
     for copy in c_p3:
         copy.wait()
     names = ("in", "post", "ffn", "out", "query", "key")
@@ -1381,19 +1383,26 @@
 
 def adam_kernel(*refs):
     ins, outs, bufs = refs[:22], refs[22:44], refs[44:66]
-    in_sems, out_sems = refs[66:]
+    last, in_sems, out_sems = refs[66:]
     loads = [pltpu.make_async_copy(src, buf, in_sems.at[at]) for at, (src, buf) in enumerate(zip(ins, bufs))]
-    stores = [pltpu.make_async_copy(buf, dst, out_sems.at[at]) for at, (buf, dst) in enumerate(zip(bufs, outs))]
+    stores = [
+        pltpu.make_async_copy(buf, dst, out_sems.at[at]) if buf.shape == dst.shape else None
+        for at, (buf, dst) in enumerate(zip(bufs, outs))
+    ]
     for load in loads:
         load.start()
     for item in range(5):
         span = range(4 * item, 4 * item + 4)
         for at in span:
             loads[at].wait()
-        stores[4 * item].start()
         grad, weight, first, second = (bufs[at] for at in span)
-        size = weight.shape[1]
-        news = adam_update(weight[...], grad[0 : weight.shape[0], 0:size], first[...], second[...])
+        given = grad[0 : weight.shape[0], 0 : weight.shape[1]]
+        if given.shape == grad.shape:
+            stores[4 * item].start()
+        else:
+            last[...] = given
+            pltpu.make_async_copy(last, outs[4 * item], out_sems.at[4 * item]).start()
+        news = adam_update(weight[...], given, first[...], second[...])
         for ref, new in zip((weight, first, second), news):
             ref[...] = new
         for at in span[1:]:
@@ -1401,30 +1410,31 @@
     for at in (20, 21):
         loads[at].wait()
         stores[at].start()
-    for store in stores:
-        store.wait()
+    for at, store in enumerate(stores):
+        if bufs[at].shape == outs[at].shape:
+            store.wait()
+        else:
+            pltpu.make_async_copy(last, outs[at], out_sems.at[at]).wait()
 
 
 def adam_call(groups, passed):
     flat = [array if array.ndim == 2 else array[None, :] for group in groups for array in group] + list(passed)
+    heads = [flat[at + 1] if at < 20 and at % 4 == 0 else array for at, array in enumerate(flat)]
     hbm = pl.BlockSpec(memory_space=pltpu.HBM)
     outs = pl.pallas_call(
         adam_kernel,
-        out_shape=[jax.ShapeDtypeStruct(array.shape, array.dtype) for array in flat],
+        out_shape=[jax.ShapeDtypeStruct(array.shape, array.dtype) for array in heads],
         in_specs=[hbm] * 22,
         out_specs=[hbm] * 22,
         scratch_shapes=[pltpu.VMEM(array.shape, array.dtype) for array in flat]
-        + [pltpu.SemaphoreType.DMA((22,)), pltpu.SemaphoreType.DMA((22,))],
+        + [pltpu.VMEM(flat[17].shape, F32), pltpu.SemaphoreType.DMA((22,)), pltpu.SemaphoreType.DMA((22,))],
         compiler_params=pltpu.CompilerParams(vmem_limit_bytes=67043328),
         name="adam",
     )(*flat)
     results = []
     for item, group in enumerate(groups):
         shape = group[1].shape
-        part = list(outs[4 * item : 4 * item + 4])
-        if part[0].shape != part[1].shape:
-            part[0] = part[0][0, : shape[0]]
-        results.append([array.reshape(shape) for array in part])
+        results.append([array.reshape(shape) for array in outs[4 * item : 4 * item + 4]])
     return results, outs[20:]
 
 

time: 170 us -> 168 us (0.988)
  no operation moved by 1% of the time
where the time goes in v1:
time: 168 us
  Pallas kernels  167 us (99%)
    pallas_call x1, Pallas kernels, backward_call(): pl.pallas_call(functools.partial(backward_kernel, dims), out_shape=[jax.S...  81.6 us
    pallas_call x1, Pallas kernels, forward_call(): pl.pallas_call(functools.partial(forward_kernel, dims), out_shape=[jax.Sh...  78.2 us
    pallas_call x1, Pallas kernels, adam_call(): pl.pallas_call(adam_kernel, out_shape=[jax.ShapeDtypeStruct(array.shape,...  6.82 us

profile of v1, /device:TPU:0, one launch (start us, length us, event | category | flops | bytes accessed | tf_op | source)
XLA Modules:
  0.0 168.1 jit_solution(1117260650570143476)
XLA Ops:
  1.3 78.2 %forward.1 = (bf16[2,4,2,2,40,256]{5,4,3,2,1,0:T(8,128)(2,1)}, bf16[2,4,2,2,40,128]{5,4,3,2,1,0:T(8,128)(2,1)}, bf16[2,4,2,2,40,128]{5,4,3,2,1,0:T(8,128)(2,1)},...) custom-call(bf16[1024,640]{1,0:T(8,128)(2,1)} %refs_24_.1, ...), custom_call_target="tpu_custom_call" | custom-call | tf_op jit(solution)/shard_map/forward/pallas_call | solution.py:959
  79.5 81.6 %backward.1 = (f32[1024,640]{1,0:T(8,128)}, f32[20,1536]{1,0:T(8,128)}, f32[32,640]{1,0:T(8,128)}, f32[20,4096]{1,0:T(8,128)}, f32[64,640]{1,0:T(8,128)}, /*index=5*/f32[8,128]{1,0:T(8,128)}) custom-call(bf16[2,640,256]{2,1,0:T(8,128)(2,1)} %bitcast.12, bf16[2,640,128]{2,1,0:T(8,128)(2,1)} %bitcast.14, bf16[2,640,128]{2,1,0:T(8,128)(2,1)} %bitcast.15, ...), custom_call_target="tpu_custom_call" | custom-call | tf_op jit(solution)/shard_map/backward/pallas_call | solution.py:1373
  161.1 6.8 %adam.1 = (f32[20,1536]{1,0:T(8,128)}, f32[20,1536]{1,0:T(8,128)}, f32[20,1536]{1,0:T(8,128)}, f32[20,1536]{1,0:T(8,128)}, f32[32,640]{1,0:T(8,128)}, /*index=5*...) custom-call(f32[20,1536]{1,0:T(8,128)} %get-tuple-element.99.refs_0_, ...), custom_call_target="tpu_custom_call" | custom-call | tf_op jit(solution)/shard_map/adam/pallas_call | solution.py:1424
